TPU v7x, 128 devices: a whole 4x4x4 slice. The times are simulated.
128 devices in a mesh: row: 16 (over z, x), col: 8 (over y, core).
Axes of the slice: x: 4, y: 4, z: 4, core: 2. Of those that a mesh axis runs over, the one named last changes fastest.
Arguments:
- panel: float32 [16, 8192, 8, 512], P('row', None, 'col'), may hold values from -1 to 4, as said below
- rhs: float32 [16, 8192, 256], P('row'), may hold values from -6 to 6
Outputs:
- solved: float32 [8, 512, 256], P('col')
- remainder: float32 [16, 8192, 256], P('row', None, 'col')
Inputs may be any that keep to these rules, and one draw needn't show every extreme that they name: panel is lower triangular in the global indices: entries with column above row are zero, diagonal entries lie between 2 and 4, the others are of size about 1 / sqrt(4096).
All inputs are finite; a program needn't handle non-finite values.
Results may differ from a plain program's by a relative error of at most 0.000084.
Values sent between devices are 32-bit elements; how exact they have to be, the bound alone decides.
A program may use at most 192 MiB of HBM per device.

v0:
```python
import jax
import jax.numpy as jnp
from jax import lax
from jax.sharding import PartitionSpec as P

TB = 512
STEPS = 8


def from_everyone(value, axis):
    copies = jnp.broadcast_to(value, (lax.axis_size(axis), *value.shape))
    return lax.all_to_all(copies, axis, split_axis=0, concat_axis=0, tiled=True)


def taken_together(value, axis):
    return from_everyone(value, axis).sum(axis=0)


def picked_2(value, axis, root):
    return lax.dynamic_index_in_dim(lax.all_gather(value, axis), root, 0, keepdims=False)


def multiply(left, right):
    return jnp.dot(left, right, precision=lax.Precision.HIGHEST, preferred_element_type=jnp.float32)


def solve_block(matrix, values):
    return lax.linalg.triangular_solve(matrix, values, left_side=True, lower=True)


def on_device(panel, rhs):
    row_count = lax.axis_size("row")
    col_count = lax.axis_size("col")
    here_row = lax.axis_index("row")
    here_col = lax.axis_index("col")
    local_panel = panel.reshape(panel.shape[1], panel.shape[3])
    right_side = rhs.reshape(rhs.shape[1], rhs.shape[2])
    identity = jnp.eye(TB, dtype=jnp.float32)
    solved = []
    for step in range(STEPS):
        owner_row = step % row_count
        owner_col = step % col_count
        tile_row = step // row_count
        tile_col = step // col_count
        row_lo = tile_row * TB
        partial_value = jnp.zeros((TB, right_side.shape[1]), jnp.float32)
        if step > 0:
            solved_stack = jnp.stack(solved)
            tile_index = 0 + here_col
            picked = lax.dynamic_index_in_dim(
                solved_stack, jnp.clip(tile_index, 0, step - 1), 0, keepdims=False
            )
            update = multiply(local_panel[row_lo : row_lo + TB, 0:TB], picked)
            partial_value = jnp.where(tile_index < step, update, 0.0)
        block_rhs = right_side[row_lo : row_lo + TB]
        summed_part = taken_together(partial_value, "col")
        is_owner = jnp.logical_and(here_row == owner_row, here_col == owner_col)
        diag_local = jnp.where(
            is_owner,
            local_panel[row_lo : row_lo + TB, tile_col * TB : (tile_col + 1) * TB],
            identity,
        )
        solution_block = picked_2(
            solve_block(diag_local, block_rhs - summed_part), "row", owner_row
        )
        solved.append(solution_block)
    solved_stack = jnp.stack(solved)
    own_blocks = lax.dynamic_index_in_dim(solved_stack, 0 + here_col, 0, keepdims=False)
    running_sum = multiply(local_panel, own_blocks)
    rhs_split = right_side.shape[1] // col_count
    reduced = lax.psum_scatter(running_sum, "col", scatter_dimension=1, tiled=True)
    own_columns = lax.dynamic_slice_in_dim(right_side, here_col * rhs_split, rhs_split, 1)
    remainder = (own_columns - reduced).reshape(1, right_side.shape[0], rhs_split)
    return (own_blocks.reshape(1, own_blocks.shape[0], own_blocks.shape[1]), remainder)


def solution(mesh):
    return jax.shard_map(
        on_device,
        mesh=mesh,
        in_specs=(P("row", None, "col", None), P("row", None, None)),
        out_specs=(P("col", None, None), P("row", None, "col")),
        check_vma=False,
    )
```

profile of v0, /device:TPU:2, one launch (start us, length us, event | category | flops | bytes accessed | tf_op | source)
XLA Modules:
  0.0 1241.3 jit_solution(1485708122632149344)
XLA Ops:
  14.3 11.4 while.16
  26.4 40.1 %custom-call.10 = f32[4,128,128]{1,2,0:T(8,128)S(1)} custom-call(f32[4,128,128]{2,1,0:T(8,128)} %copy-done.1), custom_call_target="InvertDiagBlocksLowerTriangular" | custom-call | tf_op jit(solution)/shard_map/triangular_solve/custom-call.1 | solution.py:28
  73.4 73.5 %all-gather.17.cloned.1.call-done = f32[8192,256]{1,0:T(8,128)} async-done(((f32[512,256]{1,0:T(8,128)}), f32[8192,256]{1,0:T(8,128)}) %all-gather.17.cloned.1.call-update) | async-done | bytes 8388624 | tf_op jit(solution)/shard_map/all_gather | solution.py:20
  169.3 40.1 %custom-call.11 = f32[4,128,128]{1,2,0:T(8,128)S(1)} custom-call(f32[4,128,128]{2,1,0:T(8,128)} %copy-done.2), custom_call_target="InvertDiagBlocksLowerTriangular" | custom-call | tf_op jit(solution)/shard_map/triangular_solve/custom-call.1 | solution.py:28
  219.0 69.1 %all-gather.19.cloned.1.call-done = f32[8192,256]{1,0:T(8,128)} async-done(((f32[512,256]{1,0:T(8,128)}), f32[8192,256]{1,0:T(8,128)}) %all-gather.19.cloned.1.call-update) | async-done | bytes 8388624 | tf_op jit(solution)/shard_map/all_gather | solution.py:20
  310.7 40.1 %custom-call.12 = f32[4,128,128]{1,2,0:T(8,128)S(1)} custom-call(f32[4,128,128]{2,1,0:T(8,128)} %copy-done.3), custom_call_target="InvertDiagBlocksLowerTriangular" | custom-call | tf_op jit(solution)/shard_map/triangular_solve/custom-call.1 | solution.py:28
  359.1 70.4 %all-gather.21.cloned.1.call-done = f32[8192,256]{1,0:T(8,128)} async-done(((f32[512,256]{1,0:T(8,128)}), f32[8192,256]{1,0:T(8,128)}) %all-gather.21.cloned.1.call-update) | async-done | bytes 8388624 | tf_op jit(solution)/shard_map/all_gather | solution.py:20
  441.7 11.1 while.19
  452.8 39.3 %custom-call.13 = f32[4,128,128]{1,2,0:T(8,128)S(1)} custom-call(f32[4,128,128]{2,1,0:T(8,128)S(1)} %get-tuple-element.56), custom_call_target="InvertDiagBlocksLowerTriangular" | custom-call | tf_op jit(solution)/shard_map/triangular_solve/custom-call.1 | solution.py:28
  501.5 71.0 %all-gather.23.cloned.1.call-done = f32[8192,256]{1,0:T(8,128)} async-done(((f32[512,256]{1,0:T(8,128)}), f32[8192,256]{1,0:T(8,128)}) %all-gather.23.cloned.1.call-update) | async-done | bytes 8388624 | tf_op jit(solution)/shard_map/all_gather | solution.py:20
  583.0 11.6 while.20
  594.6 39.3 %custom-call.14 = f32[4,128,128]{1,2,0:T(8,128)S(1)} custom-call(f32[4,128,128]{2,1,0:T(8,128)S(1)} %get-tuple-element.57), custom_call_target="InvertDiagBlocksLowerTriangular" | custom-call | tf_op jit(solution)/shard_map/triangular_solve/custom-call.1 | solution.py:28
  653.5 60.9 %all-gather.25.cloned.1.call-done = f32[8192,256]{1,0:T(8,128)} async-done(((f32[512,256]{1,0:T(8,128)}), f32[8192,256]{1,0:T(8,128)}) %all-gather.25.cloned.1.call-update) | async-done | bytes 8388624 | tf_op jit(solution)/shard_map/all_gather | solution.py:20
  727.3 11.1 while.21
  738.4 39.3 %custom-call.15 = f32[4,128,128]{1,2,0:T(8,128)S(1)} custom-call(f32[4,128,128]{2,1,0:T(8,128)S(1)} %get-tuple-element.58), custom_call_target="InvertDiagBlocksLowerTriangular" | custom-call | tf_op jit(solution)/shard_map/triangular_solve/custom-call.1 | solution.py:28
  787.1 71.0 %all-gather.27.cloned.1.call-done = f32[8192,256]{1,0:T(8,128)} async-done(((f32[512,256]{1,0:T(8,128)}), f32[8192,256]{1,0:T(8,128)}) %all-gather.27.cloned.1.call-update) | async-done | bytes 8388624 | tf_op jit(solution)/shard_map/all_gather | solution.py:20
  871.0 11.0 while.22
  882.1 39.3 %custom-call.16 = f32[4,128,128]{1,2,0:T(8,128)S(1)} custom-call(f32[4,128,128]{2,1,0:T(8,128)S(1)} %get-tuple-element.59), custom_call_target="InvertDiagBlocksLowerTriangular" | custom-call | tf_op jit(solution)/shard_map/triangular_solve/custom-call.1 | solution.py:28
  930.8 71.0 %all-gather.29.cloned.1.call-done = f32[8192,256]{1,0:T(8,128)} async-done(((f32[512,256]{1,0:T(8,128)}), f32[8192,256]{1,0:T(8,128)}) %all-gather.29.cloned.1.call-update) | async-done | bytes 8388624 | tf_op jit(solution)/shard_map/all_gather | solution.py:20
  1014.0 11.1 while.23
  1025.1 39.3 %custom-call.17 = f32[4,128,128]{1,2,0:T(8,128)S(1)} custom-call(f32[4,128,128]{2,1,0:T(8,128)S(1)} %get-tuple-element.60), custom_call_target="InvertDiagBlocksLowerTriangular" | custom-call | tf_op jit(solution)/shard_map/triangular_solve/custom-call.1 | solution.py:28
  1074.0 70.8 %all-gather.31.cloned.1.call-done = f32[8192,256]{1,0:T(8,128)} async-done(((f32[512,256]{1,0:T(8,128)}), f32[8192,256]{1,0:T(8,128)}) %all-gather.31.cloned.1.call-update) | async-done | bytes 8388624 | tf_op jit(solution)/shard_map/all_gather | solution.py:20
  1147.8 32.3 %fusion.3 = f32[8192,256]{0,1:T(8,128)} fusion(f32[1,8192,1,512]{3,2,1,0:T(1,128)} %param.4, f32[1,512,256]{2,1,0:T(8,128)S(1)} %constant_dynamic-slice_fusion.9), kind=kOutput, calls=%fused_computation.19 | convolution fusion | flops 12884901888 | bytes 25690112 | tf_op jit(solution)/shard_map/dot_general | solution.py:24
  1188.3 44.0 %reduce-scatter.2.cloned.1.call-done = f32[8192,32]{0,1:T(8,128)} async-done(((f32[8192,256]{0,1:T(8,128)}), f32[8192,32]{0,1:T(8,128)}) %reduce-scatter.2.cloned.1.call-update) | async-done | bytes 1048592 | tf_op jit(solution)/shard_map/reduce_scatter | solution.py:71
  (266 shorter events, 289.8 us)
Async XLA Ops:
  7.2 139.7 %all-gather.17.cloned.1.call-start = ((), (), s32[]{:S(2)}) async-start(), calls=%async_computation.9 | async-start | bytes 8912896 | tf_op jit(solution)/shard_map/all_gather | solution.py:20
  25.7 0.7 copy-start.1
  156.0 54.2 %all-to-all-start = ((f32[8,512,256]{2,1,0:T(8,128)}), f32[8,512,256]{2,1,0:T(8,128)}, u32[]{:S(2)}, u32[]{:S(2)}) async-start(f32[8,512,256]{2,1,0:T(8,128)} %broadcast_in_dim.29), calls=%async_computation | async-start | bytes 8388608 | tf_op jit(solution)/shard_map/all_to_all | solution.py:12
  160.6 127.5 %all-gather.19.cloned.1.call-start = ((), (), s32[]{:S(2)}) async-start(), calls=%async_computation.10 | async-start | bytes 8912896 | tf_op jit(solution)/shard_map/all_gather | solution.py:20
  168.5 0.7 copy-start.2
  297.3 54.2 %all-to-all-start.1 = ((f32[8,512,256]{2,1,0:T(8,128)}), f32[8,512,256]{2,1,0:T(8,128)}, u32[]{:S(2)}, u32[]{:S(2)}) async-start(f32[8,512,256]{2,1,0:T(8,128)} %broadcast_in_dim.30), calls=%async_computation.1 | async-start | bytes 8388608 | tf_op jit(solution)/shard_map/all_to_all | solution.py:12
  301.8 127.7 %all-gather.21.cloned.1.call-start = ((), (), s32[]{:S(2)}) async-start(), calls=%async_computation.11 | async-start | bytes 8912896 | tf_op jit(solution)/shard_map/all_gather | solution.py:20
  310.0 0.7 copy-start.3
  436.8 55.3 %all-to-all-start.2 = ((f32[8,512,256]{2,1,0:T(8,128)}), f32[8,512,256]{2,1,0:T(8,128)}, u32[]{:S(2)}, u32[]{:S(2)}) async-start(f32[8,512,256]{2,1,0:T(8,128)} %broadcast_in_dim.31), calls=%async_computation.2 | async-start | bytes 8388608 | tf_op jit(solution)/shard_map/all_to_all | solution.py:12
  441.4 131.1 %all-gather.23.cloned.1.call-start = ((), (), s32[]{:S(2)}) async-start(), calls=%async_computation.12 | async-start | bytes 8912896 | tf_op jit(solution)/shard_map/all_gather | solution.py:20
  578.1 55.8 %all-to-all-start.3 = ((f32[8,512,256]{2,1,0:T(8,128)}), f32[8,512,256]{2,1,0:T(8,128)}, u32[]{:S(2)}, u32[]{:S(2)}) async-start(f32[8,512,256]{2,1,0:T(8,128)} %broadcast_in_dim.32), calls=%async_computation.3 | async-start | bytes 8388608 | tf_op jit(solution)/shard_map/all_to_all | solution.py:12
  582.7 131.7 %all-gather.25.cloned.1.call-start = ((), (), s32[]{:S(2)}) async-start(), calls=%async_computation.13 | async-start | bytes 8912896 | tf_op jit(solution)/shard_map/all_gather | solution.py:20
  722.4 55.3 %all-to-all-start.4 = ((f32[8,512,256]{2,1,0:T(8,128)}), f32[8,512,256]{2,1,0:T(8,128)}, u32[]{:S(2)}, u32[]{:S(2)}) async-start(f32[8,512,256]{2,1,0:T(8,128)} %broadcast_in_dim.33), calls=%async_computation.4 | async-start | bytes 8388608 | tf_op jit(solution)/shard_map/all_to_all | solution.py:12
  727.0 131.2 %all-gather.27.cloned.1.call-start = ((), (), s32[]{:S(2)}) async-start(), calls=%async_computation.14 | async-start | bytes 8912896 | tf_op jit(solution)/shard_map/all_gather | solution.py:20
  866.0 55.5 %all-to-all-start.5 = ((f32[8,512,256]{2,1,0:T(8,128)}), f32[8,512,256]{2,1,0:T(8,128)}, u32[]{:S(2)}, u32[]{:S(2)}) async-start(f32[8,512,256]{2,1,0:T(8,128)} %broadcast_in_dim.34), calls=%async_computation.5 | async-start | bytes 8388608 | tf_op jit(solution)/shard_map/all_to_all | solution.py:12
  870.5 131.3 %all-gather.29.cloned.1.call-start = ((), (), s32[]{:S(2)}) async-start(), calls=%async_computation.15 | async-start | bytes 8912896 | tf_op jit(solution)/shard_map/all_gather | solution.py:20
  1009.4 55.0 %all-to-all-start.6 = ((f32[8,512,256]{2,1,0:T(8,128)}), f32[8,512,256]{2,1,0:T(8,128)}, u32[]{:S(2)}, u32[]{:S(2)}) async-start(f32[8,512,256]{2,1,0:T(8,128)} %broadcast_in_dim.35), calls=%async_computation.6 | async-start | bytes 8388608 | tf_op jit(solution)/shard_map/all_to_all | solution.py:12
  1014.0 130.9 %all-gather.31.cloned.1.call-start = ((), (), s32[]{:S(2)}) async-start(), calls=%async_computation.16 | async-start | bytes 8912896 | tf_op jit(solution)/shard_map/all_gather | solution.py:20
  1073.8 158.5 %reduce-scatter.2.cloned.1.call-start = ((), (), s32[]{:S(2)}) async-start(), calls=%async_computation.8 | async-start | bytes 9437184 | tf_op jit(solution)/shard_map/reduce_scatter | solution.py:71
  1147.8 32.3 %copy-start = (f32[1,512,256]{2,1,0:T(8,128)}, f32[1,512,256]{2,1,0:T(8,128)S(1)}, u32[]{:S(2)}) copy-start(f32[1,512,256]{2,1,0:T(8,128)S(1)} %constant_dynamic-slice_fusion.9) | copy-start | bytes 1572868
Sparse Core Ops, SparseCore 0:
  73.5 73.2 all-gather.16
  218.0 69.9 all-gather.18
  359.2 70.2 all-gather.20
  501.6 70.8 all-gather.22
  643.5 70.8 all-gather.24
  787.2 70.8 all-gather.26
  930.9 70.8 all-gather.28
  1073.9 70.8 all-gather.30
  1180.3 52.0 reduce-scatter.1
where the time goes:
time: 1250 us; the launch traced here: 1240 us
  waiting for transfers between devices  603 us (48%)
  other arithmetic  356 us (28%)
  local copies, waits for them, and re-layouts  145 us (12%)
  matrix products  86.5 us (7%)
  starting transfers between devices  34.4 us (3%)
  between operations  15.1 us (1%)
    all_gather x8, waiting for transfers between devices, picked_2(): lax.all_gather(value, axis)  558 us
    another operation x18, other arithmetic, solve_block(): lax.linalg.triangular_solve(matrix, values, left_side=True, lower=True)  327 us
    another operation x105, local copies, waits for them, and re-layouts, solve_block(): lax.linalg.triangular_solve(matrix, values, left_side=True, lower=True)  82 us
    dot_general x8, matrix products, multiply(): jnp.dot(left, right, precision=lax.Precision.HIGHEST, preferred_element_t...  52 us
    reduce_scatter x1, waiting for transfers between devices, on_device(): lax.psum_scatter(running_sum, 'col', scatter_dimension=1, tiled=True)  44 us
    another operation x56, matrix products, solve_block(): lax.linalg.triangular_solve(matrix, values, left_side=True, lower=True)  34.5 us
    all_to_all x7, starting transfers between devices, from_everyone(): return lax.all_to_all(copies, axis, split_axis=0, concat_axis=0, tiled=True)  31.9 us
  transfers between devices with their start and end apart: 16, of which 11 were waited for; matrix products, arithmetic and copies ran while one was open for 30% of the time, Pallas kernels for 0%

commit v1 on v0

v1 whole, which is shorter than its diff:
```python
import jax
import jax.numpy as jnp
from jax import lax
from jax.experimental import pallas as pl
from jax.experimental.pallas import tpu as pltpu
from jax.sharding import PartitionSpec as P

MESH = pl.DeviceIdType.MESH
F32 = jnp.float32
BF16 = jnp.bfloat16

TB = 512
STEPS = 8
RHS = 256
PIECE = 32
CH = 64
NCH = RHS // CH
NB = 8
BR = 1024
SIDE = 4


def split(a):
    high = a.astype(BF16)
    return high, (a - high.astype(F32)).astype(BF16)


def dot_nn(a, b):
    return jnp.dot(a, b, preferred_element_type=F32)


def dot_nt(a, b):
    return lax.dot_general(a, b, (((1,), (1,)), ((), ())), preferred_element_type=F32)


def mul(a, b):
    ah, al = split(a)
    bh, bl = split(b)
    return dot_nn(ah, bh) + (dot_nn(ah, bl) + dot_nn(al, bh))


def mul_nt(ah, al, bh, bl):
    return dot_nt(ah, bh) + (dot_nt(al, bh) + dot_nt(ah, bl))


def panel_part(full, row, count, part):
    return full[pl.ds(row * 4 + part, count, stride=4), :]


def panel_rows(full, row, count):
    return jnp.concatenate([panel_part(full, row, count, i) for i in range(4)], axis=1)


def permuted(index):
    return index % 2 * 128 + index // 2 * PIECE


def invert_diagonal(full, mh, ml):
    n = 128
    row = lax.broadcasted_iota(jnp.int32, (n, n), 0)
    col = lax.broadcasted_iota(jnp.int32, (n, n), 1)
    inverses = []
    for i in range(4):
        a = panel_part(full, i * n, n, i)
        d = jnp.where(row == col, a, 0.0)
        over_col = 1.0 / jnp.sum(d, axis=1, keepdims=True)
        over_row = 1.0 / jnp.sum(d, axis=0, keepdims=True)
        q = jnp.where(row > col, -a * over_col, 0.0)
        p = q + jnp.where(row == col, 1.0, 0.0)
        q = mul(q, q)
        for step in range(6):
            if step < 5:
                both = mul(q, jnp.concatenate([p, q], axis=1))
                p, q = p + both[:, :n], both[:, n:]
            else:
                p = p + mul(q, p)
        inverses.append(p * over_row)
    wide = []
    zero = jnp.zeros((n, n), F32)
    for i in range(2):
        first, second = inverses[2 * i], inverses[2 * i + 1]
        mid = (2 * i + 1) * n
        low = -mul(second, mul(panel_part(full, mid, n, 2 * i), first))
        wide.append(
            jnp.concatenate(
                [jnp.concatenate([first, zero], 1), jnp.concatenate([low, second], 1)], 0
            )
        )
    corner = jnp.concatenate([panel_part(full, 256, 256, 0), panel_part(full, 256, 256, 1)], 1)
    low = -mul(wide[1], mul(corner, wide[0]))
    for value, r0, c0 in ((wide[0], 0, 0), (low, 256, 0), (wide[1], 256, 256)):
        h, l = split(value)
        mh[r0 : r0 + 256, c0 : c0 + 256] = h
        ml[r0 : r0 + 256, c0 : c0 + 256] = l
    mh[0:256, 256:512] = jnp.zeros((256, 256), BF16)
    ml[0:256, 256:512] = jnp.zeros((256, 256), BF16)


def kernel(
    panel, rhs, x_out, rem_out,
    full, btile, btp, bown, mh, ml, xbuf, xh, xl, sin, sout, pt, d2, ra, fb,
    load_sem, xs, xr, ss, sr, d2s, d2r, as_, ar, bs, cs, fr,
):
    r = lax.axis_index("row")
    c = lax.axis_index("col")
    z, x = r // SIDE, r % SIDE
    y, core = c // 2, c % 2

    def load(i):
        if i == 0:
            return pltpu.make_async_copy(panel.at[pl.ds(0, 4 * TB)], full.at[pl.ds(0, 4 * TB)], load_sem.at[0])
        if i == 1:
            return pltpu.make_async_copy(rhs.at[pl.ds(0, TB)], btile, load_sem.at[1])
        if i == 2:
            rest = pl.ds(4 * TB, 4 * (NB * BR - TB))
            return pltpu.make_async_copy(panel.at[rest], full.at[rest], load_sem.at[2])
        lanes = pl.ds(pl.multiple_of(c // 4 * 128, 128), 128)
        return pltpu.make_async_copy(rhs.at[:, lanes], bown, load_sem.at[3])

    for i in range(4):
        load(i).start()

    def wrap(v):
        return (v + SIDE) % SIDE

    x_peers = (
        (z * SIDE + wrap(x + 1), c),
        (z * SIDE + wrap(x - 1), c),
        (wrap(z + 1) * SIDE + x, c),
        (wrap(z - 1) * SIDE + x, c),
    )
    partner = (r, y * 2 + 1 - core)

    def y_peer(step):
        return (r, wrap(y + step) * 2 + core)

    diagonal = (r, wrap(y + 2 * core - 1) * 2 + 1 - core)

    barrier = pltpu.get_barrier_semaphore()
    for peer in (*x_peers, partner, y_peer(1), y_peer(-1), diagonal):
        pl.semaphore_signal(barrier, inc=1, device_id=peer, device_id_type=MESH)
    pl.semaphore_wait(barrier, 8)

    dx = wrap(x - c % SIDE)
    dz = wrap(z - c // SIDE)
    has_child = (
        jnp.logical_and(dz == 0, dx <= 1),
        jnp.logical_and(dz == 0, dx == 0),
        dz <= 1,
        dz == 0,
    )
    is_diag = r == c
    is_left = jnp.logical_and(r < STEPS, c < r)

    def chunk(k):
        return pl.ds(pl.multiple_of(k * CH, CH), CH)

    def x_copy(j, k):
        return pltpu.make_async_remote_copy(
            src_ref=xbuf.at[chunk(k)], dst_ref=xbuf.at[chunk(k)],
            send_sem=xs.at[j, k], recv_sem=xr.at[k],
            device_id=x_peers[j], device_id_type=MESH,
        )

    def forward(k):
        for j in range(4):
            @pl.when(has_child[j])
            def _():
                x_copy(j, k).start()

    next_col = (r, (c + 1) % STEPS)

    def s_copy(k):
        return pltpu.make_async_remote_copy(
            src_ref=sout.at[chunk(k)], dst_ref=sin.at[chunk(k)],
            send_sem=ss.at[k], recv_sem=sr.at[k],
            device_id=next_col, device_id_type=MESH,
        )

    @pl.when(c == 0)
    def _():
        sin[...] = jnp.zeros_like(sin)

    load(0).wait()
    load(1).wait()

    @pl.when(is_diag)
    def _():
        turned = btile[...].T
        for i in range(STEPS):
            btp[permuted(i) : permuted(i) + PIECE] = turned[i * PIECE : (i + 1) * PIECE]
        invert_diagonal(full, mh, ml)

        def body(k, carry):
            @pl.when(c > 0)
            def _():
                s_copy(k).wait_recv()
            ah, al = split(btp[chunk(k)] - sin[chunk(k)])
            xbuf[chunk(k)] = mul_nt(ah, al, mh[...], ml[...])
            forward(k)
            return carry

        lax.fori_loop(0, NCH, body, 0)

    @pl.when(is_left)
    def _():
        h, l = split(panel_rows(full, 0, TB))
        mh[...] = h
        ml[...] = l

        def body(k, carry):
            x_copy(0, k).wait_recv()
            forward(k)
            ah, al = split(xbuf[chunk(k)])
            product = mul_nt(ah, al, mh[...], ml[...])

            @pl.when(c > 0)
            def _():
                s_copy(k).wait_recv()
            sout[chunk(k)] = product + sin[chunk(k)]
            s_copy(k).start()
            return carry

        lax.fori_loop(0, NCH, body, 0)

    @pl.when(jnp.logical_not(jnp.logical_or(is_diag, is_left)))
    def _():
        def body(k, carry):
            x_copy(0, k).wait_recv()
            forward(k)
            return carry

        lax.fori_loop(0, NCH, body, 0)

    h, l = split(xbuf[...])
    xh[...] = h
    xl[...] = l
    load(2).wait()

    mine = core * 128

    def rows_of(dest):
        return pl.ds(pl.multiple_of(mine + dest * PIECE, PIECE), PIECE)

    def d2_copy(t):
        return pltpu.make_async_remote_copy(
            src_ref=pt.at[t, pl.ds(pl.multiple_of(128 - mine, 128), 128)], dst_ref=d2.at[t],
            send_sem=d2s.at[t], recv_sem=d2r.at[t],
            device_id=partner, device_id_type=MESH,
        )

    def a_copy(t, way):
        return pltpu.make_async_remote_copy(
            src_ref=pt.at[t, rows_of(wrap(y + 2))], dst_ref=ra.at[t],
            send_sem=as_.at[t], recv_sem=ar.at[t],
            device_id=y_peer(way), device_id_type=MESH,
        )

    def b_copy(t, side, way):
        return pltpu.make_async_remote_copy(
            src_ref=pt.at[t, rows_of(wrap(y - way))], dst_ref=fb.at[1 - side, t],
            send_sem=bs.at[t], recv_sem=fr.at[1 - side, t],
            device_id=y_peer(-way), device_id_type=MESH,
        )

    def c_copy(t, side, way):
        return pltpu.make_async_remote_copy(
            src_ref=pt.at[t, rows_of(wrap(y + way))], dst_ref=fb.at[side, t],
            send_sem=cs.at[t], recv_sem=fr.at[side, t],
            device_id=y_peer(way), device_id_type=MESH,
        )

    def place(t):
        side, i = t % 2, t // 2
        return side, 1 - 2 * side, pl.multiple_of((side * 4 + i) * BR, BR)

    def produce(t):
        side, way, base = place(t)
        for q in range(BR // 256):
            bh, bl = split(panel_rows(full, base + q * 256, 256))
            pt[t, :, q * 256 : (q + 1) * 256] = mul_nt(xh[...], xl[...], bh, bl)
        d2_copy(t).start()

    def first_sends(t):
        side, way, base = place(t)
        d2_copy(t).wait_recv()
        own = pl.ds(pl.multiple_of(mine, 128), 128)
        pt[t, own] += d2[t]
        a_copy(t, way).start()
        b_copy(t, side, way).start()

    produce(0)

    def stage_one(t, carry):
        produce(t)
        first_sends(t - 1)
        return carry

    lax.fori_loop(1, NB, stage_one, 0)
    first_sends(NB - 1)

    x_out[...] = jnp.concatenate(
        [xbuf[permuted(i) : permuted(i) + PIECE] for i in range(STEPS)], axis=0
    ).T

    def stage_two(t, carry):
        side, way, base = place(t)
        a_copy(t, way).wait_recv()
        pt[t, rows_of(wrap(y + way))] += ra[t]
        c_copy(t, side, way).start()
        return carry

    lax.fori_loop(0, NB, stage_two, 0)

    load(3).wait()

    def stage_three(t, carry):
        side, way, base = place(t)
        c_copy(t, 0, way).wait_recv()
        c_copy(t, 1, way).wait_recv()
        turned = bown[pl.ds(base, BR)].T
        total = pt[t, rows_of(y)] + fb[0, t] + fb[1, t]
        quarter = c % 4
        chosen = turned[0:PIECE]
        for i in range(1, 4):
            chosen = jnp.where(quarter == i, turned[i * PIECE : (i + 1) * PIECE], chosen)
        rem_out[:, pl.ds(base, BR)] = chosen - total
        return carry

    lax.fori_loop(0, NB, stage_three, 0)

    def drain(t, carry):
        d2_copy(t).wait_send()
        a_copy(t, 1).wait_send()
        b_copy(t, 0, 1).wait_send()
        c_copy(t, 0, 1).wait_send()
        return carry

    lax.fori_loop(0, NB, drain, 0)

    def drain_solve(k, carry):
        for j in range(4):
            @pl.when(has_child[j])
            def _():
                x_copy(j, k).wait_send()

        @pl.when(is_left)
        def _():
            s_copy(k).wait_send()
        return carry

    lax.fori_loop(0, NCH, drain_solve, 0)


def on_device(panel, rhs):
    rows = panel.shape[1]
    panel = panel.reshape(4 * rows, 128)
    rhs = rhs.reshape(rhs.shape[1], rhs.shape[2])
    dma = pltpu.SemaphoreType.DMA
    solved, rest = pl.pallas_call(
        kernel,
        out_shape=(
            jax.ShapeDtypeStruct((TB, RHS), F32),
            jax.ShapeDtypeStruct((PIECE, rows), F32),
        ),
        in_specs=[pl.BlockSpec(memory_space=pl.ANY)] * 2,
        out_specs=(pl.BlockSpec(memory_space=pltpu.VMEM),) * 2,
        scratch_shapes=[
            pltpu.VMEM((4 * rows, 128), F32),
            pltpu.VMEM((TB, RHS), F32),
            pltpu.VMEM((RHS, TB), F32),
            pltpu.VMEM((rows, 128), F32),
            pltpu.VMEM((TB, TB), BF16),
            pltpu.VMEM((TB, TB), BF16),
            pltpu.VMEM((RHS, TB), F32),
            pltpu.VMEM((RHS, TB), BF16),
            pltpu.VMEM((RHS, TB), BF16),
            pltpu.VMEM((RHS, TB), F32),
            pltpu.VMEM((RHS, TB), F32),
            pltpu.VMEM((NB, RHS, BR), F32),
            pltpu.VMEM((NB, 128, BR), F32),
            pltpu.VMEM((NB, PIECE, BR), F32),
            pltpu.VMEM((2, NB, PIECE, BR), F32),
            dma((4,)),
            dma((4, NCH)), dma((NCH,)),
            dma((NCH,)), dma((NCH,)),
            dma((NB,)), dma((NB,)),
            dma((NB,)), dma((NB,)),
            dma((NB,)), dma((NB,)),
            dma((2, NB)),
        ],
        compiler_params=pltpu.CompilerParams(
            collective_id=0, has_side_effects=True, vmem_limit_bytes=60 * 2**20
        ),
        cost_estimate=pl.CostEstimate(
            flops=3 * 2 * rows * TB * RHS, bytes_accessed=24 * 2**20, transcendentals=0
        ),
    )(panel, rhs)
    return (solved[None], rest.T[None])


def solution(mesh):
    return jax.shard_map(
        on_device,
        mesh=mesh,
        in_specs=(P("row", None, "col", None), P("row", None, None)),
        out_specs=(P("col", None, None), P("row", None, "col")),
        check_vma=False,
    )
```

time: 1250 us -> 134 us (0.11)
  waiting for transfers between devices: 603 us -> 0 us
  other arithmetic: 356 us -> 0 us
  local copies, waits for them, and re-layouts: 145 us -> 4.13 us
  Pallas kernels: 0 us -> 127 us
  matrix products: 86.5 us -> 0 us
  starting transfers between devices: 34.4 us -> 0 us
  between operations: 15.1 us -> 0.64 us
    all_gather x8 -> x0, waiting for transfers between devices: 558 us -> none  [picked_2(): lax.all_gather(value, axis)]
    another operation x18 -> x0, other arithmetic: 327 us -> none  [solve_block(): lax.linalg.triangular_solve(matrix, values, left_side=True, lower=True)]
    pallas_call x0 -> x1, Pallas kernels: none -> 127 us  [on_device(): pl.pallas_call(kernel, out_shape=(jax.ShapeDtypeStruct((TB, RHS), F32), j...]
    another operation x107 -> x0, local copies, waits for them, and re-layouts: 85.9 us -> none  [the longest x105 82 us: solve_block(): lax.linalg.triangular_solve(matrix, values, left_side=True, lower=True)]
    dot_general x8 -> x0, matrix products: 52 us -> none  [multiply(): jnp.dot(left, right, precision=lax.Precision.HIGHEST, preferred_element_t...]
    reduce_scatter x1 -> x0, waiting for transfers between devices: 44 us -> none  [on_device(): lax.psum_scatter(running_sum, 'col', scatter_dimension=1, tiled=True)]
    another operation x56 -> x0, matrix products: 34.5 us -> none  [solve_block(): lax.linalg.triangular_solve(matrix, values, left_side=True, lower=True)]
    all_to_all x7 -> x0, starting transfers between devices: 31.9 us -> none  [from_everyone(): return lax.all_to_all(copies, axis, split_axis=0, concat_axis=0, tiled=True)]
  transfers between devices with their start and end apart: 16 -> 0, of which waited for: 11 -> 0; matrix products, arithmetic and copies ran while one was open for 30% -> 0% of each run, Pallas kernels for 0% -> 0%
where the time goes in v1:
time: 134 us; the launch traced here: 132 us
  Pallas kernels  127 us (95%)
  local copies, waits for them, and re-layouts  4.13 us (3%)
    pallas_call x1, Pallas kernels, on_device(): pl.pallas_call(kernel, out_shape=(jax.ShapeDtypeStruct((TB, RHS), F32), j...  127 us
    unnamed x2, local copies, waits for them, and re-layouts  4.13 us

profile of v1, /device:TPU:2, one launch (start us, length us, event | category | flops | bytes accessed | tf_op | source)
XLA Modules:
  0.0 132.2 jit_solution(11322172157638551269)
XLA Ops:
  0.6 127.4 %shard_map.41 = (f32[512,256]{1,0:T(8,128)}, f32[32,8192]{1,0:T(8,128)}) custom-call(f32[32768,128]{1,0:T(8,128)} %bitcast.6, f32[8192,256]{1,0:T(8,128)} %bitcast.7), custom_call_target="tpu_custom_call" | custom-call | flops 6442450944 | bytes 25165824 | tf_op jit(solution)/shard_map/pallas_call | solution.py:360
  128.1 1.9 %copy.6 = f32[1,512,256]{2,1,0:T(8,128)} copy(f32[1,512,256]{2,1,0:T(8,128)} %bitcast.9) | data formatting | bytes 1048576
  129.9 2.3 %copy.7 = f32[1,8192,32]{1,2,0:T(8,128)} copy(f32[1,8192,32]{1,2,0:T(8,128)} %bitcast.8) | data formatting | bytes 2097152

commit v2 on v1

--- a/solution.py
+++ b/solution.py
@@ -13,10 +13,14 @@
 STEPS = 8
 RHS = 256
 PIECE = 32
-CH = 64
+CH = 16
 NCH = RHS // CH
-NB = 8
-BR = 1024
+NG = 1
+GR = RHS // NG
+GP = PIECE // NG
+NBK = 8
+BC = 8192 // NBK
+NT = NG * NBK
 SIDE = 4
 
 
@@ -39,8 +43,14 @@
     return dot_nn(ah, bh) + (dot_nn(ah, bl) + dot_nn(al, bh))
 
 
-def mul_nt(ah, al, bh, bl):
-    return dot_nt(ah, bh) + (dot_nt(al, bh) + dot_nt(ah, bl))
+def mul_nt(stacked, bh, bl):
+    n = stacked.shape[0] // 2
+    both = dot_nt(stacked, bh)
+    return both[:n] + (both[n:] + dot_nt(stacked[:n], bl))
+
+
+def stack(a):
+    return jnp.concatenate(split(a), axis=0)
 
 
 def panel_part(full, row, count, part):
@@ -51,8 +61,8 @@
     return jnp.concatenate([panel_part(full, row, count, i) for i in range(4)], axis=1)
 
 
-def permuted(index):
-    return index % 2 * 128 + index // 2 * PIECE
+def permuted(device, group):
+    return group * GR + device % 2 * (GR // 2) + device // 2 * GP
 
 
 def invert_diagonal(full, mh, ml):
@@ -98,13 +108,14 @@
 
 def kernel(
     panel, rhs, x_out, rem_out,
-    full, btile, btp, bown, mh, ml, xbuf, xh, xl, sin, sout, pt, d2, ra, fb,
+    full, lh, ll, btile, btp, bown, bturn, mh, ml, xbuf, x2, sin, sout, pt, d2, ra, fb,
     load_sem, xs, xr, ss, sr, d2s, d2r, as_, ar, bs, cs, fr,
 ):
     r = lax.axis_index("row")
     c = lax.axis_index("col")
     z, x = r // SIDE, r % SIDE
     y, core = c // 2, c % 2
+    rows = NBK * BC
 
     def load(i):
         if i == 0:
@@ -112,13 +123,13 @@
         if i == 1:
             return pltpu.make_async_copy(rhs.at[pl.ds(0, TB)], btile, load_sem.at[1])
         if i == 2:
-            rest = pl.ds(4 * TB, 4 * (NB * BR - TB))
+            rest = pl.ds(4 * TB, 4 * (rows - TB))
             return pltpu.make_async_copy(panel.at[rest], full.at[rest], load_sem.at[2])
         lanes = pl.ds(pl.multiple_of(c // 4 * 128, 128), 128)
         return pltpu.make_async_copy(rhs.at[:, lanes], bown, load_sem.at[3])
 
-    for i in range(4):
-        load(i).start()
+    load(0).start()
+    load(1).start()
 
     def wrap(v):
         return (v + SIDE) % SIDE
@@ -143,14 +154,21 @@
 
     dx = wrap(x - c % SIDE)
     dz = wrap(z - c // SIDE)
-    has_child = (
-        jnp.logical_and(dz == 0, dx <= 1),
-        jnp.logical_and(dz == 0, dx == 0),
-        dz <= 1,
-        dz == 0,
-    )
+
+    def along(d):
+        up = jnp.logical_or(d == 0, jnp.logical_and(d == 1, core == 1))
+        down = jnp.logical_or(d == 0, jnp.logical_and(d == 3, core == 0))
+        return up, down
+
+    def has_child(j, k):
+        if j < 2:
+            return jnp.logical_and(along(dx)[j], jnp.logical_or(dz == 0, k % 2 == 1))
+        return jnp.logical_and(along(dz)[j - 2], jnp.logical_or(dx == 0, k % 2 == 0))
+
     is_diag = r == c
     is_left = jnp.logical_and(r < STEPS, c < r)
+    ahead = jnp.logical_or(jnp.logical_or(is_left, is_diag), c < STEPS - 2)
+    passes = jnp.logical_not(jnp.logical_or(is_left, is_diag))
 
     def chunk(k):
         return pl.ds(pl.multiple_of(k * CH, CH), CH)
@@ -164,7 +182,7 @@
 
     def forward(k):
         for j in range(4):
-            @pl.when(has_child[j])
+            @pl.when(has_child(j, k))
             def _():
                 x_copy(j, k).start()
 
@@ -183,24 +201,17 @@
 
     load(0).wait()
     load(1).wait()
+    load(2).start()
+    load(3).start()
 
     @pl.when(is_diag)
     def _():
         turned = btile[...].T
         for i in range(STEPS):
-            btp[permuted(i) : permuted(i) + PIECE] = turned[i * PIECE : (i + 1) * PIECE]
+            for g in range(NG):
+                at = permuted(i, g)
+                btp[at : at + GP] = turned[i * PIECE + g * GP : i * PIECE + (g + 1) * GP]
         invert_diagonal(full, mh, ml)
-
-        def body(k, carry):
-            @pl.when(c > 0)
-            def _():
-                s_copy(k).wait_recv()
-            ah, al = split(btp[chunk(k)] - sin[chunk(k)])
-            xbuf[chunk(k)] = mul_nt(ah, al, mh[...], ml[...])
-            forward(k)
-            return carry
-
-        lax.fori_loop(0, NCH, body, 0)
 
     @pl.when(is_left)
     def _():
@@ -208,43 +219,81 @@
         mh[...] = h
         ml[...] = l
 
-        def body(k, carry):
-            x_copy(0, k).wait_recv()
-            forward(k)
-            ah, al = split(xbuf[chunk(k)])
-            product = mul_nt(ah, al, mh[...], ml[...])
-
-            @pl.when(c > 0)
-            def _():
-                s_copy(k).wait_recv()
-            sout[chunk(k)] = product + sin[chunk(k)]
-            s_copy(k).start()
+    load(2).wait()
+    load(3).wait()
+
+    def prepare():
+        def body(i, carry):
+            at = pl.multiple_of(i * 256, 256)
+            h, l = split(panel_rows(full, at, 256))
+            lh[pl.ds(at, 256)] = h
+            ll[pl.ds(at, 256)] = l
+            turned = bown[pl.ds(at, 256)].T
+            quarter = c % 4
+            chosen = turned[0:PIECE]
+            for j in range(1, 4):
+                chosen = jnp.where(quarter == j, turned[j * PIECE : (j + 1) * PIECE], chosen)
+            bturn[:, pl.ds(at, 256)] = chosen
             return carry
 
-        lax.fori_loop(0, NCH, body, 0)
-
-    @pl.when(jnp.logical_not(jnp.logical_or(is_diag, is_left)))
-    def _():
-        def body(k, carry):
-            x_copy(0, k).wait_recv()
-            forward(k)
-            return carry
-
-        lax.fori_loop(0, NCH, body, 0)
-
-    h, l = split(xbuf[...])
-    xh[...] = h
-    xl[...] = l
-    load(2).wait()
-
-    mine = core * 128
+        lax.fori_loop(0, rows // 256, body, 0)
+
+    early = c >= 2
+
+    @pl.when(early)
+    def _():
+        prepare()
+
+    def own_chunk(k, carry):
+        @pl.when(c > 0)
+        def _():
+            s_copy(k).wait_recv()
+        xbuf[chunk(k)] = mul_nt(stack(btp[chunk(k)] - sin[chunk(k)]), mh[...], ml[...])
+        forward(k)
+        return carry
+
+    def left_chunk(k, carry):
+        x_copy(0, k).wait_recv()
+        forward(k)
+        product = mul_nt(stack(xbuf[chunk(k)]), mh[...], ml[...])
+
+        @pl.when(c > 0)
+        def _():
+            s_copy(k).wait_recv()
+        sout[chunk(k)] = product + sin[chunk(k)]
+        s_copy(k).start()
+        return carry
+
+    def passed_chunk(k, carry):
+        x_copy(0, k).wait_recv()
+        forward(k)
+        return carry
+
+    @pl.when(is_diag)
+    def _():
+        lax.fori_loop(0, NCH, own_chunk, 0)
+
+    @pl.when(is_left)
+    def _():
+        lax.fori_loop(0, NCH, left_chunk, 0)
+
+    @pl.when(jnp.logical_and(passes, ahead))
+    def _():
+        lax.fori_loop(0, NCH, passed_chunk, 0)
+
+    @pl.when(jnp.logical_not(early))
+    def _():
+        prepare()
+
+    mine = core * (GR // 2)
 
     def rows_of(dest):
-        return pl.ds(pl.multiple_of(mine + dest * PIECE, PIECE), PIECE)
+        return pl.ds(pl.multiple_of(mine + dest * GP, GP), GP)
 
     def d2_copy(t):
-        return pltpu.make_async_remote_copy(
-            src_ref=pt.at[t, pl.ds(pl.multiple_of(128 - mine, 128), 128)], dst_ref=d2.at[t],
+        other = pl.ds(pl.multiple_of(GR // 2 - mine, GR // 2), GR // 2)
+        return pltpu.make_async_remote_copy(
+            src_ref=pt.at[t, other], dst_ref=d2.at[t],
             send_sem=d2s.at[t], recv_sem=d2r.at[t],
             device_id=partner, device_id_type=MESH,
         )
@@ -271,63 +320,81 @@
         )
 
     def place(t):
-        side, i = t % 2, t // 2
-        return side, 1 - 2 * side, pl.multiple_of((side * 4 + i) * BR, BR)
-
-    def produce(t):
+        side, i = t % 2, t % NBK // 2
+        return side, 1 - 2 * side, pl.multiple_of((side * (NBK // 2) + i) * BC, BC)
+
+    def produce(g, t):
         side, way, base = place(t)
-        for q in range(BR // 256):
-            bh, bl = split(panel_rows(full, base + q * 256, 256))
-            pt[t, :, q * 256 : (q + 1) * 256] = mul_nt(xh[...], xl[...], bh, bl)
+        wide = min(BC, 1024)
+
+        def body(q, carry):
+            for s in range(wide // 256):
+                at = pl.multiple_of(q * wide + s * 256, 256)
+                part = pl.ds(base + at, 256)
+                pt[t, :, pl.ds(at, 256)] = mul_nt(x2[g], lh[part], ll[part])
+            return carry
+
+        lax.fori_loop(0, BC // wide, body, 0)
         d2_copy(t).start()
 
     def first_sends(t):
         side, way, base = place(t)
         d2_copy(t).wait_recv()
-        own = pl.ds(pl.multiple_of(mine, 128), 128)
+        own = pl.ds(pl.multiple_of(mine, GR // 2), GR // 2)
         pt[t, own] += d2[t]
         a_copy(t, way).start()
         b_copy(t, side, way).start()
 
-    produce(0)
-
-    def stage_one(t, carry):
-        produce(t)
-        first_sends(t - 1)
-        return carry
-
-    lax.fori_loop(1, NB, stage_one, 0)
-    first_sends(NB - 1)
-
-    x_out[...] = jnp.concatenate(
-        [xbuf[permuted(i) : permuted(i) + PIECE] for i in range(STEPS)], axis=0
-    ).T
-
-    def stage_two(t, carry):
+    def second_sends(t, carry):
         side, way, base = place(t)
         a_copy(t, way).wait_recv()
         pt[t, rows_of(wrap(y + way))] += ra[t]
         c_copy(t, side, way).start()
         return carry
 
-    lax.fori_loop(0, NB, stage_two, 0)
-
-    load(3).wait()
-
-    def stage_three(t, carry):
+    def one_group(g, carry):
+        per = NCH // NG
+
+        @pl.when(jnp.logical_not(ahead))
+        def _():
+            lax.fori_loop(g * per, (g + 1) * per, passed_chunk, 0)
+
+        x2[g] = stack(xbuf[pl.ds(pl.multiple_of(g * GR, GR), GR)])
+        first = g * NBK
+        produce(g, first)
+
+        def stage(i, carry):
+            produce(g, first + i)
+            first_sends(first + i - 1)
+            return carry
+
+        lax.fori_loop(1, NBK, stage, 0)
+        first_sends(first + NBK - 1)
+
+        @pl.when(g > 0)
+        def _():
+            lax.fori_loop(first - NBK, first, second_sends, 0)
+        return carry
+
+    lax.fori_loop(0, NG, one_group, 0)
+    lax.fori_loop(NT - NBK, NT, second_sends, 0)
+
+    pieces = []
+    for i in range(STEPS):
+        for g in range(NG):
+            pieces.append(xbuf[permuted(i, g) : permuted(i, g) + GP])
+    x_out[...] = jnp.concatenate(pieces, axis=0).T
+
+    def finish(t, carry):
         side, way, base = place(t)
         c_copy(t, 0, way).wait_recv()
         c_copy(t, 1, way).wait_recv()
-        turned = bown[pl.ds(base, BR)].T
         total = pt[t, rows_of(y)] + fb[0, t] + fb[1, t]
-        quarter = c % 4
-        chosen = turned[0:PIECE]
-        for i in range(1, 4):
-            chosen = jnp.where(quarter == i, turned[i * PIECE : (i + 1) * PIECE], chosen)
-        rem_out[:, pl.ds(base, BR)] = chosen - total
-        return carry
-
-    lax.fori_loop(0, NB, stage_three, 0)
+        at = (pl.ds(pl.multiple_of(t // NBK * GP, GP), GP), pl.ds(base, BC))
+        rem_out[at] = bturn[at] - total
+        return carry
+
+    lax.fori_loop(0, NT, finish, 0)
 
     def drain(t, carry):
         d2_copy(t).wait_send()
@@ -336,11 +403,11 @@
         c_copy(t, 0, 1).wait_send()
         return carry
 
-    lax.fori_loop(0, NB, drain, 0)
+    lax.fori_loop(0, NT, drain, 0)
 
     def drain_solve(k, carry):
         for j in range(4):
-            @pl.when(has_child[j])
+            @pl.when(has_child(j, k))
             def _():
                 x_copy(j, k).wait_send()
 
@@ -367,30 +434,32 @@
         out_specs=(pl.BlockSpec(memory_space=pltpu.VMEM),) * 2,
         scratch_shapes=[
             pltpu.VMEM((4 * rows, 128), F32),
+            pltpu.VMEM((rows, TB), BF16),
+            pltpu.VMEM((rows, TB), BF16),
             pltpu.VMEM((TB, RHS), F32),
             pltpu.VMEM((RHS, TB), F32),
             pltpu.VMEM((rows, 128), F32),
+            pltpu.VMEM((PIECE, rows), F32),
             pltpu.VMEM((TB, TB), BF16),
             pltpu.VMEM((TB, TB), BF16),
             pltpu.VMEM((RHS, TB), F32),
-            pltpu.VMEM((RHS, TB), BF16),
-            pltpu.VMEM((RHS, TB), BF16),
+            pltpu.VMEM((NG, 2 * GR, TB), BF16),
             pltpu.VMEM((RHS, TB), F32),
             pltpu.VMEM((RHS, TB), F32),
-            pltpu.VMEM((NB, RHS, BR), F32),
-            pltpu.VMEM((NB, 128, BR), F32),
-            pltpu.VMEM((NB, PIECE, BR), F32),
-            pltpu.VMEM((2, NB, PIECE, BR), F32),
+            pltpu.VMEM((NT, GR, BC), F32),
+            pltpu.VMEM((NT, GR // 2, BC), F32),
+            pltpu.VMEM((NT, GP, BC), F32),
+            pltpu.VMEM((2, NT, GP, BC), F32),
             dma((4,)),
             dma((4, NCH)), dma((NCH,)),
             dma((NCH,)), dma((NCH,)),
-            dma((NB,)), dma((NB,)),
-            dma((NB,)), dma((NB,)),
-            dma((NB,)), dma((NB,)),
-            dma((2, NB)),
+            dma((NT,)), dma((NT,)),
+            dma((NT,)), dma((NT,)),
+            dma((NT,)), dma((NT,)),
+            dma((2, NT)),
         ],
         compiler_params=pltpu.CompilerParams(
-            collective_id=0, has_side_effects=True, vmem_limit_bytes=60 * 2**20
+            collective_id=0, has_side_effects=True, vmem_limit_bytes=63 * 2**20
         ),
         cost_estimate=pl.CostEstimate(
             flops=3 * 2 * rows * TB * RHS, bytes_accessed=24 * 2**20, transcendentals=0

time: 134 us -> 112 us (0.84); the launches traced: 132 us -> 112 us
  Pallas kernels: 127 us -> 107 us
    pallas_call x1, Pallas kernels: 127 us -> 107 us  [on_device(): pl.pallas_call(kernel, out_shape=(jax.ShapeDtypeStruct((TB, RHS), F32), j...]
where the time goes in v2:
time: 112 us
  Pallas kernels  107 us (96%)
  local copies, waits for them, and re-layouts  4.13 us (4%)
    pallas_call x1, Pallas kernels, on_device(): pl.pallas_call(kernel, out_shape=(jax.ShapeDtypeStruct((TB, RHS), F32), j...  107 us
    unnamed x2, local copies, waits for them, and re-layouts  4.13 us

profile of v2, /device:TPU:2, one launch (start us, length us, event | category | flops | bytes accessed | tf_op | source)
XLA Modules:
  0.0 111.8 jit_solution(5242727015743225555)
XLA Ops:
  0.6 107.1 %shard_map.41 = (f32[512,256]{1,0:T(8,128)}, f32[32,8192]{1,0:T(8,128)}) custom-call(f32[32768,128]{1,0:T(8,128)} %bitcast.6, f32[8192,256]{1,0:T(8,128)} %bitcast.7), custom_call_target="tpu_custom_call" | custom-call | flops 6442450944 | bytes 25165824 | tf_op jit(solution)/shard_map/pallas_call | solution.py:427
  107.7 1.9 %copy.6 = f32[1,512,256]{2,1,0:T(8,128)} copy(f32[1,512,256]{2,1,0:T(8,128)} %bitcast.9) | data formatting | bytes 1048576
  109.6 2.3 %copy.7 = f32[1,8192,32]{1,2,0:T(8,128)} copy(f32[1,8192,32]{1,2,0:T(8,128)} %bitcast.8) | data formatting | bytes 2097152

commit v3 on v2

--- a/solution.py
+++ b/solution.py
@@ -38,9 +38,15 @@
 
 
 def mul(a, b):
-    ah, al = split(a)
     bh, bl = split(b)
-    return dot_nn(ah, bh) + (dot_nn(ah, bl) + dot_nn(al, bh))
+    stacked = stack(a)
+    n = a.shape[0]
+    both = dot_nn(stacked, bh)
+    return both[:n] + (both[n:] + dot_nn(stacked[:n], bl))
+
+
+def mul_once(a, b):
+    return dot_nn(a.astype(BF16), b.astype(BF16))
 
 
 def mul_nt(stacked, bh, bl):
@@ -80,10 +86,10 @@
         q = mul(q, q)
         for step in range(6):
             if step < 5:
-                both = mul(q, jnp.concatenate([p, q], axis=1))
+                both = (mul if step < 3 else mul_once)(q, jnp.concatenate([p, q], axis=1))
                 p, q = p + both[:, :n], both[:, n:]
             else:
-                p = p + mul(q, p)
+                p = p + mul_once(q, p)
         inverses.append(p * over_row)
     wide = []
     zero = jnp.zeros((n, n), F32)
@@ -150,7 +156,6 @@
     barrier = pltpu.get_barrier_semaphore()
     for peer in (*x_peers, partner, y_peer(1), y_peer(-1), diagonal):
         pl.semaphore_signal(barrier, inc=1, device_id=peer, device_id_type=MESH)
-    pl.semaphore_wait(barrier, 8)
 
     dx = wrap(x - c % SIDE)
     dz = wrap(z - c // SIDE)
@@ -219,10 +224,12 @@
         mh[...] = h
         ml[...] = l
 
-    load(2).wait()
-    load(3).wait()
+    pl.semaphore_wait(barrier, 8)
 
     def prepare():
+        load(2).wait()
+        load(3).wait()
+
         def body(i, carry):
             at = pl.multiple_of(i * 256, 256)
             h, l = split(panel_rows(full, at, 256))
@@ -427,8 +434,8 @@
     solved, rest = pl.pallas_call(
         kernel,
         out_shape=(
-            jax.ShapeDtypeStruct((TB, RHS), F32),
-            jax.ShapeDtypeStruct((PIECE, rows), F32),
+            pltpu.VMEM((TB, RHS), F32),
+            pltpu.VMEM((PIECE, rows), F32),
         ),
         in_specs=[pl.BlockSpec(memory_space=pl.ANY)] * 2,
         out_specs=(pl.BlockSpec(memory_space=pltpu.VMEM),) * 2,
@@ -459,7 +466,7 @@
             dma((2, NT)),
         ],
         compiler_params=pltpu.CompilerParams(
-            collective_id=0, has_side_effects=True, vmem_limit_bytes=63 * 2**20
+            collective_id=0, has_side_effects=True, vmem_limit_bytes=60 * 2**20
         ),
         cost_estimate=pl.CostEstimate(
             flops=3 * 2 * rows * TB * RHS, bytes_accessed=24 * 2**20, transcendentals=0

time: 112 us -> 104 us (0.929)
  Pallas kernels: 107 us -> 101 us
  local copies, waits for them, and re-layouts: 4.13 us -> 1.77 us
    pallas_call x1, Pallas kernels: 107 us -> 101 us  [on_device(): pl.pallas_call(kernel, out_shape=(pltpu.VMEM((TB, RHS), F32), pltpu.VMEM(...]
    unnamed x2, local copies, waits for them, and re-layouts: 4.13 us -> 1.77 us
where the time goes in v3:
time: 104 us
  Pallas kernels  101 us (97%)
  local copies, waits for them, and re-layouts  1.77 us (2%)
    pallas_call x1, Pallas kernels, on_device(): pl.pallas_call(kernel, out_shape=(pltpu.VMEM((TB, RHS), F32), pltpu.VMEM(...  101 us

profile of v3, /device:TPU:2, one launch (start us, length us, event | category | flops | bytes accessed | tf_op | source)
XLA Modules:
  0.0 103.8 jit_solution(15239694550587382634)
XLA Ops:
  0.6 101.4 %shard_map.41 = (f32[512,256]{1,0:T(8,128)S(1)}, f32[32,8192]{1,0:T(8,128)S(1)}) custom-call(f32[32768,128]{1,0:T(8,128)} %bitcast.8, f32[8192,256]{1,0:T(8,128)} %bitcast.9), custom_call_target="tpu_custom_call" | custom-call | flops 6442450944 | bytes 25165824 | tf_op jit(solution)/shard_map/pallas_call | solution.py:434
  102.1 0.8 copy.6
  102.9 1.0 copy.7

commit v4 on v3

--- a/solution.py
+++ b/solution.py
@@ -1,3 +1,5 @@
+import functools
+
 import jax
 import jax.numpy as jnp
 from jax import lax
@@ -18,7 +20,7 @@
 NG = 1
 GR = RHS // NG
 GP = PIECE // NG
-NBK = 8
+NBK = 16
 BC = 8192 // NBK
 NT = NG * NBK
 SIDE = 4
@@ -424,6 +426,17 @@
         return carry
 
     lax.fori_loop(0, NCH, drain_solve, 0)
+
+
+def hand_over(solved, rest, solved_out, rest_out, sem):
+    copies = (
+        pltpu.make_async_copy(solved, solved_out, sem.at[0]),
+        pltpu.make_async_copy(rest, rest_out, sem.at[1]),
+    )
+    for copy in copies:
+        copy.start()
+    for copy in copies:
+        copy.wait()
 
 
 def on_device(panel, rhs):
@@ -472,6 +485,18 @@
             flops=3 * 2 * rows * TB * RHS, bytes_accessed=24 * 2**20, transcendentals=0
         ),
     )(panel, rhs)
+    keep = functools.partial(pltpu.with_memory_space_constraint, memory_space=pltpu.VMEM)
+    solved, rest = pl.pallas_call(
+        hand_over,
+        out_shape=(
+            jax.ShapeDtypeStruct((TB, RHS), F32),
+            jax.ShapeDtypeStruct((PIECE, rows), F32),
+        ),
+        in_specs=[pl.BlockSpec(memory_space=pltpu.VMEM)] * 2,
+        out_specs=(pl.BlockSpec(memory_space=pl.ANY),) * 2,
+        scratch_shapes=[dma((2,))],
+        compiler_params=pltpu.CompilerParams(vmem_limit_bytes=2**20),
+    )(keep(solved), keep(rest))
     return (solved[None], rest.T[None])
 
 

time: 104 us -> 103 us (level)
  local copies, waits for them, and re-layouts: 1.77 us -> 0 us
    unnamed x2 -> x0, local copies, waits for them, and re-layouts: 1.77 us -> none
    pallas_call x0 -> x1, Pallas kernels: none -> 1.16 us  [on_device(): pl.pallas_call(hand_over, out_shape=(jax.ShapeDtypeStruct((TB, RHS), F32)...]
where the time goes in v4:
time: 103 us
  Pallas kernels  102 us (99%)
    pallas_call x1, Pallas kernels, on_device(): pl.pallas_call(kernel, out_shape=(pltpu.VMEM((TB, RHS), F32), pltpu.VMEM(...  101 us

profile of v4, /device:TPU:2, one launch (start us, length us, event | category | flops | bytes accessed | tf_op | source)
XLA Modules:
  0.0 103.0 jit_solution(4435414246237353461)
XLA Ops:
  0.6 101.2 %shard_map.41 = (f32[512,256]{1,0:T(8,128)S(1)}, f32[32,8192]{1,0:T(8,128)S(1)}) custom-call(f32[32768,128]{1,0:T(8,128)} %bitcast.6, f32[8192,256]{1,0:T(8,128)} %bitcast.7), custom_call_target="tpu_custom_call" | custom-call | flops 6442450944 | bytes 25165824 | tf_op jit(solution)/shard_map/pallas_call | solution.py:447
  101.9 1.2 %shard_map.42 = (f32[512,256]{1,0:T(8,128)}, f32[32,8192]{1,0:T(8,128)}) custom-call(f32[512,256]{1,0:T(8,128)S(1)} %get-tuple-element.6.solved, f32[32,8192]{1,0:T(8,128)S(1)} %get-tuple-element.7.rest), custom_call_target="tpu_custom_call" | custom-call | tf_op jit(solution)/shard_map/pallas_call | solution.py:489

commit v5 on v4

--- a/solution.py
+++ b/solution.py
@@ -453,7 +453,7 @@
         in_specs=[pl.BlockSpec(memory_space=pl.ANY)] * 2,
         out_specs=(pl.BlockSpec(memory_space=pltpu.VMEM),) * 2,
         scratch_shapes=[
-            pltpu.VMEM((4 * rows, 128), F32),
+            pltpu.VMEM((4 * rows + 8, 128), F32),
             pltpu.VMEM((rows, TB), BF16),
             pltpu.VMEM((rows, TB), BF16),
             pltpu.VMEM((TB, RHS), F32),

time: 103 us -> 103 us (level)
  no operation moved by 1% of the time
where the time goes in v5:
time: 103 us
  Pallas kernels  102 us (99%)
    pallas_call x1, Pallas kernels, on_device(): pl.pallas_call(kernel, out_shape=(pltpu.VMEM((TB, RHS), F32), pltpu.VMEM(...  101 us

profile of v5, /device:TPU:2, one launch (start us, length us, event | category | flops | bytes accessed | tf_op | source)
XLA Modules:
  0.0 103.0 jit_solution(6958433014595186827)
XLA Ops:
  0.6 101.2 %shard_map.41 = (f32[512,256]{1,0:T(8,128)S(1)}, f32[32,8192]{1,0:T(8,128)S(1)}) custom-call(f32[32768,128]{1,0:T(8,128)} %bitcast.6, f32[8192,256]{1,0:T(8,128)} %bitcast.7), custom_call_target="tpu_custom_call" | custom-call | flops 6442450944 | bytes 25165824 | tf_op jit(solution)/shard_map/pallas_call | solution.py:447
  101.9 1.2 %shard_map.42 = (f32[512,256]{1,0:T(8,128)}, f32[32,8192]{1,0:T(8,128)}) custom-call(f32[512,256]{1,0:T(8,128)S(1)} %get-tuple-element.6.solved, f32[32,8192]{1,0:T(8,128)S(1)} %get-tuple-element.7.rest), custom_call_target="tpu_custom_call" | custom-call | tf_op jit(solution)/shard_map/pallas_call | solution.py:489
